TPU v7x, 32 devices: a whole 2x2x4 slice. The times are simulated.
32 devices in a mesh: row: 4 (over y, x), col: 4 (over z), rep: 2 (over core).
Axes of the slice: x: 2, y: 2, z: 4, core: 2. Of those that a mesh axis runs over, the one named last changes fastest.
Arguments:
- sources: int32 [64], replicated, may hold values from 0 to 4095
- tile_weights: int32 [1024, 128, 128], P(('row', 'col', 'rep')), may hold values from 0 to 16, as said below
- tile_src: int32 [1024], P(('row', 'col', 'rep')), may hold values from 0 to 31, as said below
- tile_dst: int32 [1024], P(('row', 'col', 'rep')), may hold values from 0 to 31, as said below
- tile_count: int32 [32], P(('row', 'col', 'rep')), may hold values from 1 to 32, 512 in all
Outputs:
- distances: float32 [64, 4096], P(None, ('row', 'col', 'rep'))
- recip_sums: float32 [16, 64], P(('row', 'col'))
Inputs may be any that keep to these rules, and one draw needn't show every extreme that they name: `tile_weights`: an entry of 0 means no edge; others are the edge's weight. `tile_src`: piece p = b // 1 of block b belongs to the device at mesh coordinates (row, col, rep) = (p // 8, (p // 2) % 4, p % 2); slot k belongs to device k // 32 in the same numbering. A tile's source block lies in a piece whose col index is that of the tile's device. `tile_dst`: A tile's destination block lies in a piece whose row and rep indices are those of the tile's device, in the numbering given for tile_src. Only the first tile_count[d] slots of device d hold live tiles; some device has all 32 slots live.
All inputs are finite; a program needn't handle non-finite values.
Results may differ from a plain program's by a relative error of at most 0.0003.
Values may be sent and summed in bfloat16 or wider, within the bound.
No kernel may reach another device: no remote copies, remote signals or barrier semaphores. Data moves between devices by JAX's collectives and lax.ppermute only.
A program may use at most 64 MiB of HBM per device.

v0:
```python
import jax
import jax.numpy as jnp
from jax import lax
from jax.sharding import PartitionSpec as P

BLK_DEV = 1
TILE_DEV = 32
BS = 128
ROUNDS = 2
far_value = 255.0


def relax_tiles(gathered, weights, src_pos, dst_pos, ordering, live_total, blocks_out):
    height = gathered.shape[0]
    partial_value = jnp.full((height, blocks_out * BS), far_value, jnp.bfloat16)

    def relax_four(step_no, partial_value):
        for offset in range(4):
            slot_now = 4 * step_no + offset
            picked = ordering[slot_now]
            weight = lax.dynamic_index_in_dim(weights, picked, 0, keepdims=False)
            source = lax.dynamic_slice_in_dim(gathered, src_pos[picked] * BS, BS, 1)
            candidate = jnp.min(source[:, :, None] + weight[None, :, :], axis=1)
            candidate = jnp.where(slot_now < live_total, candidate, jnp.bfloat16(far_value))
            begin_at = dst_pos[picked] * BS
            previous = lax.dynamic_slice_in_dim(partial_value, begin_at, BS, 1)
            partial_value = lax.dynamic_update_slice_in_dim(
                partial_value, jnp.minimum(previous, candidate), begin_at, 1
            )
        return partial_value

    return lax.fori_loop(0, (live_total + 3) // 4, relax_four, partial_value)


def source_slot(block_ids, n_col, n_rep):
    piece_id = block_ids // BLK_DEV
    return (piece_id // (n_col * n_rep) * n_rep + piece_id % n_rep) * BLK_DEV + block_ids % BLK_DEV


def per_device(sources, tile_weights, tile_src, tile_dst, tile_count):
    n_col = lax.axis_size("col")
    n_rep = lax.axis_size("rep")
    width = BLK_DEV * BS
    sources_all = sources.shape[0]
    piece_id = (lax.axis_index("row") * n_col + lax.axis_index("col")) * n_rep + lax.axis_index(
        "rep"
    )
    columns = piece_id * width + jnp.arange(width, dtype=jnp.int32)
    dist = jnp.where(columns[None, :] == sources[:, None], 0.0, far_value).astype(jnp.bfloat16)
    weights = jnp.where(tile_weights > 0, tile_weights.astype(jnp.float32), far_value).astype(
        jnp.bfloat16
    )
    ordering = jnp.arange(TILE_DEV, dtype=jnp.int32)
    live_total = tile_count[0]
    src_pos = source_slot(tile_src, n_col, n_rep)
    dest_piece = tile_dst // BLK_DEV
    dst_pos = dest_piece // n_rep % n_col * BLK_DEV + tile_dst % BLK_DEV
    for round_no in range(ROUNDS):
        gathered = lax.all_gather(dist, ("row", "rep"), axis=1, tiled=True)
        partial_value = relax_tiles(
            gathered, weights, src_pos, dst_pos, ordering, live_total, n_col * BLK_DEV
        )
        fresh = jnp.min(
            lax.all_to_all(
                partial_value.reshape(sources_all, 1, n_col * width),
                "col",
                split_axis=2,
                concat_axis=1,
                tiled=True,
            ),
            axis=1,
        )
        dist = jnp.minimum(dist, fresh)
    as_float = dist.astype(jnp.float32)
    inverse = jnp.where(as_float > 0, 1.0 / jnp.maximum(as_float, 1.0), 0.0)
    sums = lax.psum(jnp.sum(inverse, axis=1), "rep")
    return (as_float, sums[None, :])


def solution(mesh):
    return jax.shard_map(
        per_device,
        mesh=mesh,
        in_specs=(
            P(),
            P(("row", "col", "rep"), None, None),
            P(("row", "col", "rep")),
            P(("row", "col", "rep")),
            P(("row", "col", "rep")),
        ),
        out_specs=(P(None, ("row", "col", "rep")), P(("row", "col"), None)),
        check_vma=False,
    )
```

profile of v0, /device:TPU:0, one launch (start us, length us, event | category | flops | bytes accessed | tf_op | source)
XLA Modules:
  0.0 407.2 jit_solution(2897030421059010277)
XLA Ops:
  2.1 10.5 %all_gather.6 = bf16[64,1024]{1,0:T(8,128)(2,1)S(1)} all-gather(bf16[64,128]{1,0:T(8,128)(2,1)S(1)} %select_convert_fusion.1), channel_id=1, replica_groups=mesh['row'=4,'col'=4,'rep'=2] {'row','rep'}, dimensions={1}, use_global_device_ids=true | all-gather | bytes 147456 | tf_op jit(solution)/shard_map/all_gather | solution.py:59
  12.6 2.6 select_convert_fusion
  15.3 178.3 %while.26 = (s32[]{:T(128)}, bf16[64,512]{1,0:T(8,128)(2,1)S(1)}, s32[]{:T(128)}, s32[32]{0:T(128)S(1)}, s32[32]{0:T(128)S(1)}, /*index=5*/s32[]{:T(128)}, s32[3...) while((s32[]{:T(128)}, bf16[64,512]{1,0:T(8,128)(2,1)S(1)}, ...), condition=%wide.region_5.6_spmd.clone, body=%wide.region_0.5_spmd.clone.sunk | while | flops 8519746 | bytes 853061 | solution.py:32
  26.9 1.4 add_reduce_fusion.18
  28.2 1.4 add_reduce_fusion.17
  29.6 1.4 add_reduce_fusion.16
  34.9 1.4 add_reduce_fusion.19
  49.2 1.4 add_reduce_fusion.18
  50.5 1.4 add_reduce_fusion.17
  51.9 1.4 add_reduce_fusion.16
  57.1 1.4 add_reduce_fusion.19
  71.4 1.4 add_reduce_fusion.18
  72.8 1.4 add_reduce_fusion.17
  74.2 1.4 add_reduce_fusion.16
  79.4 1.4 add_reduce_fusion.19
  93.7 1.4 add_reduce_fusion.18
  95.1 1.4 add_reduce_fusion.17
  96.5 1.4 add_reduce_fusion.16
  101.7 1.4 add_reduce_fusion.19
  116.0 1.4 add_reduce_fusion.18
  117.4 1.4 add_reduce_fusion.17
  118.8 1.4 add_reduce_fusion.16
  124.0 1.4 add_reduce_fusion.19
  138.3 1.4 add_reduce_fusion.18
  139.7 1.4 add_reduce_fusion.17
  141.1 1.4 add_reduce_fusion.16
  146.3 1.4 add_reduce_fusion.19
  160.6 1.4 add_reduce_fusion.18
  162.0 1.4 add_reduce_fusion.17
  168.6 1.4 add_reduce_fusion.19
  182.9 1.4 add_reduce_fusion.18
  184.3 1.4 add_reduce_fusion.17
  185.6 1.4 add_reduce_fusion.16
  190.9 1.4 add_reduce_fusion.19
  194.3 1.4 reduce.4
  196.5 4.9 %all-to-all-start = ((bf16[4,2,4096]{2,1,0:T(2,128)(2,1)}), bf16[4,2,4096]{2,1,0:T(2,128)(2,1)S(1)}, u32[]{:S(2)}, u32[]{:S(2)}) async-start(bf16[4,2,4096]{2,1,0:T(2,128)(2,1)} %reshape.63), calls=%async_computation | async-start | bytes 131072 | tf_op jit(solution)/shard_map/all_to_all | solution.py:64
  201.4 5.7 %all-to-all-done = bf16[4,2,4096]{2,1,0:T(2,128)(2,1)S(1)} async-done(((bf16[4,2,4096]{2,1,0:T(2,128)(2,1)}), bf16[4,2,4096]{2,1,0:T(2,128)(2,1)S(1)}, u32[]{:S(2)}, u32[]{:S(2)}) %all-to-all-start) | async-done | bytes 65568 | tf_op jit(solution)/shard_map/all_to_all | solution.py:64
  207.6 7.6 %all_gather.7 = bf16[64,1024]{1,0:T(8,128)(2,1)S(1)} all-gather(bf16[64,128]{1,0:T(8,128)(2,1)S(1)} %fusion), channel_id=1, replica_groups=mesh['row'=4,'col'=4,'rep'=2] {'row','rep'}, dimensions={1}, use_global_device_ids=true | all-gather | bytes 147456 | tf_op jit(solution)/shard_map/all_gather | solution.py:59
  215.2 177.9 %while.27 = (s32[]{:T(128)}, bf16[64,512]{1,0:T(8,128)(2,1)S(1)}, s32[]{:T(128)}, s32[32]{0:T(128)S(1)}, s32[32]{0:T(128)S(1)}, /*index=5*/s32[]{:T(128)}, s32[3...) while((s32[]{:T(128)}, bf16[64,512]{1,0:T(8,128)(2,1)S(1)}, ...), condition=%wide.region_12.13_spmd.clone, body=%wide.region_7.12_spmd.clone.sunk | while | flops 8519746 | bytes 853061 | solution.py:32
  226.7 1.4 add_reduce_fusion.22
  228.1 1.4 add_reduce_fusion.21
  234.7 1.4 add_reduce_fusion.23
  250.4 1.4 add_reduce_fusion.21
  257.0 1.4 add_reduce_fusion.23
  272.6 1.4 add_reduce_fusion.21
  279.2 1.4 add_reduce_fusion.23
  293.5 1.4 add_reduce_fusion.22
  294.8 1.4 add_reduce_fusion.21
  296.2 1.4 add_reduce_fusion.20
  301.4 1.4 add_reduce_fusion.23
  315.7 1.4 add_reduce_fusion.22
  317.1 1.4 add_reduce_fusion.21
  318.4 1.4 add_reduce_fusion.20
  337.9 1.4 add_reduce_fusion.22
  340.7 1.4 add_reduce_fusion.20
  360.2 1.4 add_reduce_fusion.22
  362.9 1.4 add_reduce_fusion.20
  368.2 1.4 add_reduce_fusion.23
  382.4 1.4 add_reduce_fusion.22
  385.1 1.4 add_reduce_fusion.20
  390.4 1.4 add_reduce_fusion.23
  393.3 1.4 reduce.5
  394.9 8.1 %all_to_all.24 = bf16[4,2,4096]{2,1,0:T(2,128)(2,1)S(1)} all-to-all(bf16[4,2,4096]{2,1,0:T(2,128)(2,1)S(1)} %reshape.65), channel_id=1, replica_groups=mesh['row'=4,'col'=4,'rep'=2] {'col'}, dimensions={0} | all-to-all | bytes 131072 | tf_op jit(solution)/shard_map/all_to_all | solution.py:64
  404.2 3.0 psum.7
  (167 shorter events, 43.6 us)
Async XLA Ops:
  0.6 14.6 %copy-start.2 = (s32[32]{0:T(128)S(1)}, s32[32]{0:T(128)}, u32[]{:S(2)}) copy-start(s32[32]{0:T(128)} %param.11) | copy-start | bytes 388
  0.6 14.6 %copy-start.1 = (s32[32]{0:T(128)S(1)}, s32[32]{0:T(128)}, u32[]{:S(2)}) copy-start(s32[32]{0:T(128)} %param.12) | copy-start | bytes 388
  15.3 192.2 %copy-start = (s32[64]{0:T(128)S(1)}, s32[64]{0:T(128)}, u32[]{:S(2)}) copy-start(s32[64]{0:T(128)} %param.9) | copy-start | bytes 772
  196.5 10.6 %all-to-all-start = ((bf16[4,2,4096]{2,1,0:T(2,128)(2,1)}), bf16[4,2,4096]{2,1,0:T(2,128)(2,1)S(1)}, u32[]{:S(2)}, u32[]{:S(2)}) async-start(bf16[4,2,4096]{2,1,0:T(2,128)(2,1)} %reshape.63), calls=%async_computation | async-start | bytes 131072 | tf_op jit(solution)/shard_map/all_to_all | solution.py:64
where the time goes:
time: 411 us; the launch traced here: 407 us
  loops' own time  244 us (59%)
  other arithmetic  96 us (23%)
  blocking collectives  29.2 us (7%)
  local copies, waits for them, and re-layouts  25.5 us (6%)
  waiting for transfers between devices  5.74 us (1%)
  starting transfers between devices  4.87 us (1%)
    another operation x2, loops' own time, relax_tiles(): return lax.fori_loop(0, (live_total + 3) // 4, relax_four, partial_value)  244 us
    reduce_min x64, other arithmetic, relax_four(): candidate = jnp.min(source[:, :, None] + weight[None, :, :], axis=1)  87.5 us
    all_gather x2, blocking collectives, per_device(): gathered = lax.all_gather(dist, ('row', 'rep'), axis=1, tiled=True)  18.1 us
    dynamic_slice x32, local copies, waits for them, and re-layouts, relax_four(): source = lax.dynamic_slice_in_dim(gathered, src_pos[picked] * BS, BS, 1)  11.8 us
    dynamic_slice x16, local copies, waits for them, and re-layouts, relax_four(): picked = ordering[slot_now]  11 us
  transfers between devices with their start and end apart: 1, of which 1 were waited for; matrix products, arithmetic and copies ran while one was open for 0% of the time, Pallas kernels for 0%

commit v1 on v0

--- a/solution.py
+++ b/solution.py
@@ -8,6 +8,22 @@
 BS = 128
 ROUNDS = 2
 far_value = 255.0
+
+
+def swapped_with_each(x, axis, split, join):
+    ways, here = (lax.axis_size(axis), lax.axis_index(axis))
+    width = x.shape[split] // ways
+    lengths = list(x.shape)
+    lengths[split] = width
+    height = lengths[join]
+    lengths[join] = height * ways
+    full = jnp.zeros(lengths, x.dtype)
+    for mask in range(ways):
+        part = lax.dynamic_slice_in_dim(x, (here ^ mask) * width, width, axis=split)
+        if mask:
+            part = lax.ppermute(part, axis, [(d, d ^ mask) for d in range(ways)])
+        full = lax.dynamic_update_slice_in_dim(full, part, (here ^ mask) * height, axis=join)
+    return full
 
 
 def relax_tiles(gathered, weights, src_pos, dst_pos, ordering, live_total, blocks_out):
@@ -61,13 +77,7 @@
             gathered, weights, src_pos, dst_pos, ordering, live_total, n_col * BLK_DEV
         )
         fresh = jnp.min(
-            lax.all_to_all(
-                partial_value.reshape(sources_all, 1, n_col * width),
-                "col",
-                split_axis=2,
-                concat_axis=1,
-                tiled=True,
-            ),
+            swapped_with_each(partial_value.reshape(sources_all, 1, n_col * width), "col", 2, 1),
             axis=1,
         )
         dist = jnp.minimum(dist, fresh)

time: 411 us -> 404 us (0.983)
  blocking collectives: 29.2 us -> 21.1 us
    ppermute x0 -> x6, starting transfers between devices: none -> 8.95 us  [swapped_with_each(): part = lax.ppermute(part, axis, [(d, d ^ mask) for d in range(ways)])]
    ppermute x0 -> x6, waiting for transfers between devices: none -> 8.22 us  [swapped_with_each(): part = lax.ppermute(part, axis, [(d, d ^ mask) for d in range(ways)])]
    all_to_all x1 -> x0, blocking collectives: 8.11 us -> none  [per_device(): lax.all_to_all(partial_value.reshape(sources_all, 1, n_col * width), 'col...]
    all_to_all x1 -> x0, waiting for transfers between devices: 5.74 us -> none  [per_device(): lax.all_to_all(partial_value.reshape(sources_all, 1, n_col * width), 'col...]
    all_to_all x1 -> x0, starting transfers between devices: 4.87 us -> none  [per_device(): lax.all_to_all(partial_value.reshape(sources_all, 1, n_col * width), 'col...]
  transfers between devices with their start and end apart: 1 -> 6, of which waited for: 1 -> 4; matrix products, arithmetic and copies ran while one was open for 0% -> 0% of each run, Pallas kernels for 0% -> 0%
where the time goes in v1:
time: 404 us; the launch traced here: 401 us
  loops' own time  245 us (61%)
  other arithmetic  93.1 us (23%)
  local copies, waits for them, and re-layouts  23.3 us (6%)
  blocking collectives  21.1 us (5%)
  starting transfers between devices  8.95 us (2%)
  waiting for transfers between devices  8.22 us (2%)
    another operation x2, loops' own time, relax_tiles(): return lax.fori_loop(0, (live_total + 3) // 4, relax_four, partial_value)  245 us
    reduce_min x64, other arithmetic, relax_four(): candidate = jnp.min(source[:, :, None] + weight[None, :, :], axis=1)  87.5 us
    all_gather x2, blocking collectives, per_device(): gathered = lax.all_gather(dist, ('row', 'rep'), axis=1, tiled=True)  18.1 us
    dynamic_slice x32, local copies, waits for them, and re-layouts, relax_four(): source = lax.dynamic_slice_in_dim(gathered, src_pos[picked] * BS, BS, 1)  11.8 us
    dynamic_slice x16, local copies, waits for them, and re-layouts, relax_four(): picked = ordering[slot_now]  11 us
    ppermute x6, starting transfers between devices, swapped_with_each(): part = lax.ppermute(part, axis, [(d, d ^ mask) for d in range(ways)])  8.95 us
    ppermute x6, waiting for transfers between devices, swapped_with_each(): part = lax.ppermute(part, axis, [(d, d ^ mask) for d in range(ways)])  8.22 us
  transfers between devices with their start and end apart: 6, of which 4 were waited for; matrix products, arithmetic and copies ran while one was open for 0% of the time, Pallas kernels for 0%

profile of v1, /device:TPU:0, one launch (start us, length us, event | category | flops | bytes accessed | tf_op | source)
XLA Modules:
  0.0 400.9 jit_solution(3491207965316013446)
XLA Ops:
  2.1 10.5 %all_gather.6 = bf16[64,1024]{1,0:T(8,128)(2,1)S(1)} all-gather(bf16[64,128]{1,0:T(8,128)(2,1)S(1)} %select_convert_fusion.1), channel_id=1, replica_groups=mesh['row'=4,'col'=4,'rep'=2] {'row','rep'}, dimensions={1}, use_global_device_ids=true | all-gather | bytes 147456 | tf_op jit(solution)/shard_map/all_gather | solution.py:75
  12.6 2.6 select_convert_fusion
  15.3 178.3 %while.26 = (s32[]{:T(128)}, bf16[64,512]{1,0:T(8,128)(2,1)S(1)}, s32[]{:T(128)}, s32[32]{0:T(128)S(1)}, s32[32]{0:T(128)S(1)}, /*index=5*/s32[]{:T(128)}, s32[3...) while((s32[]{:T(128)}, bf16[64,512]{1,0:T(8,128)(2,1)S(1)}, ...), condition=%wide.region_5.6_spmd.clone, body=%wide.region_0.5_spmd.clone.sunk | while | flops 8519746 | bytes 853061 | solution.py:48
  26.9 1.4 add_reduce_fusion.18
  28.3 1.4 add_reduce_fusion.17
  29.6 1.4 add_reduce_fusion.16
  34.9 1.4 add_reduce_fusion.19
  49.2 1.4 add_reduce_fusion.18
  50.5 1.4 add_reduce_fusion.17
  51.9 1.4 add_reduce_fusion.16
  57.2 1.4 add_reduce_fusion.19
  71.5 1.4 add_reduce_fusion.18
  72.8 1.4 add_reduce_fusion.17
  74.2 1.4 add_reduce_fusion.16
  79.4 1.4 add_reduce_fusion.19
  93.7 1.4 add_reduce_fusion.18
  95.1 1.4 add_reduce_fusion.17
  96.5 1.4 add_reduce_fusion.16
  101.7 1.4 add_reduce_fusion.19
  116.0 1.4 add_reduce_fusion.18
  117.4 1.4 add_reduce_fusion.17
  118.8 1.4 add_reduce_fusion.16
  124.0 1.4 add_reduce_fusion.19
  139.7 1.4 add_reduce_fusion.17
  146.3 1.4 add_reduce_fusion.19
  162.0 1.4 add_reduce_fusion.17
  168.6 1.4 add_reduce_fusion.19
  182.9 1.4 add_reduce_fusion.18
  184.3 1.4 add_reduce_fusion.17
  185.6 1.4 add_reduce_fusion.16
  190.9 1.4 add_reduce_fusion.19
  193.8 4.2 %collective-permute-start.1 = (bf16[64,1,128]{2,0,1:T(8,128)(2,1)S(1)}, bf16[64,1,128]{2,0,1:T(8,128)(2,1)S(1)}, u32[]{:S(2)}, u32[]{:S(2)}) collective-permute-start(bf16[64,1,128]{2,0,1:T(8,128)(2,1)S(1)} %get-tuple-element.398), channel_id=1, source_target_pairs={{0,4},{2,6},{4,0},{6,2},{1,5},{3,7},{5,1},{7,3},{8,12},{10,14},{12... | collective-permute-start | bytes 49160 | tf_op jit(solution)/shard_map/ppermute | solution.py:24
  198.2 1.4 collective-permute-done.1
  199.6 3.8 collective-permute-done.2
  203.6 7.6 %all_gather.7 = bf16[64,1024]{1,0:T(8,128)(2,1)S(1)} all-gather(bf16[64,128]{1,0:T(8,128)(2,1)S(1)} %fusion), channel_id=1, replica_groups=mesh['row'=4,'col'=4,'rep'=2] {'row','rep'}, dimensions={1}, use_global_device_ids=true | all-gather | bytes 147456 | tf_op jit(solution)/shard_map/all_gather | solution.py:75
  211.2 178.3 %while.27 = (s32[]{:T(128)}, bf16[64,512]{1,0:T(8,128)(2,1)S(1)}, s32[]{:T(128)}, s32[32]{0:T(128)S(1)}, s32[32]{0:T(128)S(1)}, /*index=5*/s32[]{:T(128)}, s32[3...) while((s32[]{:T(128)}, bf16[64,512]{1,0:T(8,128)(2,1)S(1)}, ...), condition=%wide.region_12.13_spmd.clone, body=%wide.region_7.12_spmd.clone.sunk | while | flops 8519746 | bytes 853061 | solution.py:48
  222.7 1.4 add_reduce_fusion.22
  225.5 1.4 add_reduce_fusion.20
  230.7 1.4 add_reduce_fusion.23
  245.0 1.4 add_reduce_fusion.22
  246.4 1.4 add_reduce_fusion.21
  247.8 1.4 add_reduce_fusion.20
  253.0 1.4 add_reduce_fusion.23
  268.7 1.4 add_reduce_fusion.21
  275.3 1.4 add_reduce_fusion.23
  289.6 1.4 add_reduce_fusion.22
  291.0 1.4 add_reduce_fusion.21
  292.3 1.4 add_reduce_fusion.20
  311.9 1.4 add_reduce_fusion.22
  314.6 1.4 add_reduce_fusion.20
  319.9 1.4 add_reduce_fusion.23
  334.2 1.4 add_reduce_fusion.22
  335.5 1.4 add_reduce_fusion.21
  336.9 1.4 add_reduce_fusion.20
  342.1 1.4 add_reduce_fusion.23
  357.8 1.4 add_reduce_fusion.21
  364.4 1.4 add_reduce_fusion.23
  378.7 1.4 add_reduce_fusion.22
  380.1 1.4 add_reduce_fusion.21
  381.5 1.4 add_reduce_fusion.20
  389.6 1.9 collective-permute-start.4
  391.5 2.5 collective-permute-start.5
  394.3 2.7 collective-permute-done.5
  397.9 3.0 psum.7
  (175 shorter events, 43.3 us)
Async XLA Ops:
  0.6 14.6 %copy-start.2 = (s32[32]{0:T(128)S(1)}, s32[32]{0:T(128)}, u32[]{:S(2)}) copy-start(s32[32]{0:T(128)} %param.11) | copy-start | bytes 388
  0.6 14.6 %copy-start.1 = (s32[32]{0:T(128)S(1)}, s32[32]{0:T(128)}, u32[]{:S(2)}) copy-start(s32[32]{0:T(128)} %param.12) | copy-start | bytes 388
  15.3 188.2 %copy-start = (s32[64]{0:T(128)S(1)}, s32[64]{0:T(128)}, u32[]{:S(2)}) copy-start(s32[64]{0:T(128)} %param.9) | copy-start | bytes 772
  193.7 4.5 %collective-permute-start = (bf16[64,1,128]{2,0,1:T(8,128)(2,1)S(1)}, bf16[64,1,128]{2,0,1:T(8,128)(2,1)S(1)}, u32[]{:S(2)}, u32[]{:S(2)}) collective-permute-start(bf16[64,1,128]{2,0,1:T(8,128)(2,1)S(1)} %get-tuple-element.399), channel_id=1, source_target_pairs={{0,2},{2,0},{4,6},{6,4},{1,3},{3,1},{5,7},{7,5},{8,10},{10,8},{12,... | collective-permute-start | bytes 49160 | tf_op jit(solution)/shard_map/ppermute | solution.py:24
  193.8 5.9 %collective-permute-start.1 = (bf16[64,1,128]{2,0,1:T(8,128)(2,1)S(1)}, bf16[64,1,128]{2,0,1:T(8,128)(2,1)S(1)}, u32[]{:S(2)}, u32[]{:S(2)}) collective-permute-start(bf16[64,1,128]{2,0,1:T(8,128)(2,1)S(1)} %get-tuple-element.398), channel_id=1, source_target_pairs={{0,4},{2,6},{4,0},{6,2},{1,5},{3,7},{5,1},{7,3},{8,12},{10,14},{12... | collective-permute-start | bytes 49160 | tf_op jit(solution)/shard_map/ppermute | solution.py:24
  197.9 5.5 %collective-permute-start.2 = (bf16[64,1,128]{2,0,1:T(8,128)(2,1)S(1)}, bf16[64,1,128]{2,0,1:T(8,128)(2,1)S(1)}, u32[]{:S(2)}, u32[]{:S(2)}) collective-permute-start(bf16[64,1,128]{2,0,1:T(8,128)(2,1)S(1)} %get-tuple-element.397), channel_id=1, source_target_pairs={{0,6},{2,4},{4,2},{6,0},{1,7},{3,5},{5,3},{7,1},{8,14},{10,12},{12... | collective-permute-start | bytes 49160 | tf_op jit(solution)/shard_map/ppermute | solution.py:24
  389.5 4.6 %collective-permute-start.3 = (bf16[64,1,128]{2,0,1:T(8,128)(2,1)S(1)}, bf16[64,1,128]{2,0,1:T(8,128)(2,1)S(1)}, u32[]{:S(2)}, u32[]{:S(2)}) collective-permute-start(bf16[64,1,128]{2,0,1:T(8,128)(2,1)S(1)} %get-tuple-element.396), channel_id=1, source_target_pairs={{0,2},{2,0},{4,6},{6,4},{1,3},{3,1},{5,7},{7,5},{8,10},{10,8},{12,... | collective-permute-start | bytes 49160 | tf_op jit(solution)/shard_map/ppermute | solution.py:24
  389.6 4.7 %collective-permute-start.4 = (bf16[64,1,128]{2,0,1:T(8,128)(2,1)S(1)}, bf16[64,1,128]{2,0,1:T(8,128)(2,1)S(1)}, u32[]{:S(2)}, u32[]{:S(2)}) collective-permute-start(bf16[64,1,128]{2,0,1:T(8,128)(2,1)S(1)} %get-tuple-element.395), channel_id=1, source_target_pairs={{0,4},{2,6},{4,0},{6,2},{1,5},{3,7},{5,1},{7,3},{8,12},{10,14},{12... | collective-permute-start | bytes 49160 | tf_op jit(solution)/shard_map/ppermute | solution.py:24
  391.5 5.5 %collective-permute-start.5 = (bf16[64,1,128]{2,0,1:T(8,128)(2,1)S(1)}, bf16[64,1,128]{2,0,1:T(8,128)(2,1)S(1)}, u32[]{:S(2)}, u32[]{:S(2)}) collective-permute-start(bf16[64,1,128]{2,0,1:T(8,128)(2,1)S(1)} %get-tuple-element.394), channel_id=1, source_target_pairs={{0,6},{2,4},{4,2},{6,0},{1,7},{3,5},{5,3},{7,1},{8,14},{10,12},{12... | collective-permute-start | bytes 49160 | tf_op jit(solution)/shard_map/ppermute | solution.py:24
